TPU v7x, 32 devices: a whole 2x2x4 slice. The times are simulated.
32 devices in a mesh: row: 4 (over y, x), col: 8 (over z, core).
Axes of the slice: x: 2, y: 2, z: 4, core: 2. Of those that a mesh axis runs over, the one named last changes fastest.
Arguments:
- pair_rep: bfloat16 [96, 96, 128], P('row', 'col'), may hold values from -6 to 6
- pair_mask: int32 [96, 96], P('row', 'col'), may hold values 0 or 1
- proj_weight: bfloat16 [2, 5, 128, 128], replicated, may hold values from -0.5 to 0.5
- out_weight: bfloat16 [2, 128, 128], replicated, may hold values from -0.5 to 0.5
- norm_gain: float32 [2, 2, 128], replicated, may hold values from 0.25 to 1.75
- norm_bias: float32 [2, 2, 128], replicated, may hold values from -1.5 to 1.5
Outputs:
- pair_out: bfloat16 [96, 96, 128], P('row', 'col')
Inputs may be any that keep to these rules, and one draw needn't show every extreme that they name: pair_mask holds only 0 and 1.
All inputs are finite; a program needn't handle non-finite values.
Results may differ from a plain program's by a relative error of at most 0.0095.
Values may be sent and summed in bfloat16 or wider, within the bound.
A program may use at most 64 MiB of HBM per device.

v0:
```python
import jax
import jax.numpy as jnp
from jax import lax
from jax.sharding import PartitionSpec as P

epsilon = 1e-05


def scattered(term, extent, axis):
    whole = term(jnp.int32(0), extent * lax.axis_size(axis))
    return lax.psum_scatter(whole, axis, scatter_dimension=0, tiled=True)


def layer_norm(values, gain_vec, bias_vec):
    average = jnp.mean(values, axis=-1, keepdims=True)
    centred = values - average
    variance = jnp.mean(centred * centred, axis=-1, keepdims=True)
    return centred * lax.rsqrt(variance + epsilon) * gain_vec + bias_vec


def projections(pair_rep, mask_float, proj_weight, norm_gain, norm_bias, layer_no):
    channels = pair_rep.shape[2]
    normed = layer_norm(
        pair_rep.astype(jnp.float32), norm_gain[layer_no, 0], norm_bias[layer_no, 0]
    ).astype(jnp.bfloat16)
    flattened = normed.reshape(-1, channels)
    products = [
        jnp.dot(
            flattened, proj_weight[layer_no, which], preferred_element_type=jnp.float32
        ).reshape(pair_rep.shape)
        for which in range(5)
    ]
    left_side = (jax.nn.sigmoid(products[0]) * products[1] * mask_float).astype(jnp.bfloat16)
    right_side = (jax.nn.sigmoid(products[2]) * products[3] * mask_float).astype(jnp.bfloat16)
    gate_value = jax.nn.sigmoid(products[4])
    return (left_side, right_side, gate_value)


def finish(pair_rep, triangle, gate_value, out_weight, norm_gain, norm_bias, layer_no):
    channels = pair_rep.shape[2]
    normed = layer_norm(triangle, norm_gain[layer_no, 1], norm_bias[layer_no, 1]).astype(
        jnp.bfloat16
    )
    projected = jnp.dot(
        normed.reshape(-1, channels), out_weight[layer_no], preferred_element_type=jnp.float32
    ).reshape(pair_rep.shape)
    return (pair_rep.astype(jnp.float32) + gate_value * projected).astype(jnp.bfloat16)


def shards(pair_rep, pair_mask, proj_weight, out_weight, norm_gain, norm_bias):
    rows_dev, cols_dev, channels = pair_rep.shape
    mask_float = pair_mask.astype(jnp.float32)[..., None]
    left_side, right_side, gate_value = projections(
        pair_rep, mask_float, proj_weight, norm_gain, norm_bias, 0
    )
    right_all = lax.all_gather(right_side, "row", axis=0, tiled=True)

    def outgoing_term(first_idx, how_many):
        sliced = lax.dynamic_slice_in_dim(right_all, first_idx, how_many, 0)
        return jnp.einsum("jkc,ikc->jic", sliced, left_side, preferred_element_type=jnp.float32)

    triangle = scattered(outgoing_term, cols_dev, "col")
    triangle = jnp.transpose(triangle, (1, 0, 2))
    pair_rep = finish(pair_rep, triangle, gate_value, out_weight, norm_gain, norm_bias, 0)
    left_side, right_side, gate_value = projections(
        pair_rep, mask_float, proj_weight, norm_gain, norm_bias, 1
    )
    left_all = lax.all_gather(left_side, "col", axis=1, tiled=True)

    def incoming_term(first_idx, how_many):
        sliced = lax.dynamic_slice_in_dim(left_all, first_idx, how_many, 1)
        return jnp.einsum("kic,kjc->ijc", sliced, right_side, preferred_element_type=jnp.float32)

    triangle = scattered(incoming_term, rows_dev, "row")
    pair_rep = finish(pair_rep, triangle, gate_value, out_weight, norm_gain, norm_bias, 1)
    return pair_rep


def solution(mesh):
    in_specs = (P("row", "col", None), P("row", "col"), P(), P(), P(), P())
    out_specs = P("row", "col", None)
    return jax.shard_map(shards, mesh=mesh, in_specs=in_specs, out_specs=out_specs, check_vma=False)
```

profile of v0, /device:TPU:0, one launch (start us, length us, event | category | flops | bytes accessed | tf_op | source)
XLA Modules:
  0.0 137.0 jit_solution(15166773543570996231)
XLA Ops:
  6.5 1.0 convert_reduce_fusion
  7.5 1.1 fusion.39
  8.6 0.8 slice_bitcast_fusion
  9.4 1.2 fusion.60
  10.6 1.2 fusion.57
  11.8 0.7 convert_element_type.43
  12.5 1.2 fusion.34
  13.7 1.2 fusion.33
  14.8 11.0 %all_gather.6 = bf16[96,12,128]{2,0,1:T(8,128)(2,1)S(1)} all-gather(bf16[24,12,128]{2,0,1:T(8,128)(2,1)S(1)} %fusion.33), channel_id=1, replica_groups=mesh['row'=4,'col'=8] {'row'}, dimensions={0}, use_global_device_ids=true | all-gather | bytes 368640 | tf_op jit(solution)/shard_map/all_gather | solution.py:56
  25.8 0.4 copy.44
  26.3 0.4 copy.43
  26.7 0.6 convolution_bitcast_fusion
  27.4 1.6 %copy.45 = f32[96,24,128]{2,1,0:T(8,128)} copy(f32[96,24,128]{0,1,2:T(8,128)S(1)} %convolution_bitcast_fusion) | data formatting | bytes 2359296 | tf_op jit(solution)/shard_map/jkc,ikc->jic/transpose | solution.py:60
  29.0 33.3 %reduce-scatter.3.cloned.1.call-done = f32[12,24,128]{2,1,0:T(8,128)} async-done(((f32[96,24,128]{2,1,0:T(8,128)}), f32[12,24,128]{2,1,0:T(8,128)}) %reduce-scatter.3.cloned.1.call-update) | async-done | bytes 147472 | tf_op jit(solution)/shard_map/reduce_scatter | solution.py:11
  62.3 1.0 bitcast_reduce_fusion
  63.3 1.1 multiply_reduce_fusion.2
  64.5 1.2 fusion.43
  65.7 1.1 fusion.83
  67.2 0.9 fusion.50
  68.1 0.9 fusion.53
  69.0 1.0 fusion.30
  70.0 1.0 fusion.31
  71.0 1.2 copy.50
  72.2 15.8 %all_gather.7 = bf16[24,96,128]{2,0,1:T(8,128)(2,1)} all-gather(bf16[24,12,128]{2,0,1:T(8,128)(2,1)S(1)} %fusion.30), channel_id=1, replica_groups=mesh['row'=4,'col'=8] {'col'}, dimensions={1}, use_global_device_ids=true | all-gather | bytes 663552 | tf_op jit(solution)/shard_map/all_gather | solution.py:68
  88.0 5.2 %copy.51 = bf16[24,96,128]{0,1,2:T(8,128)(2,1)S(1)} copy(bf16[24,96,128]{2,0,1:T(8,128)(2,1)} %all_gather.7) | data formatting | bytes 1179648 | tf_op jit(solution)/shard_map/all_gather | solution.py:68
  93.3 3.8 %convolution_bitcast_fusion.1 = f32[96,12,128]{0,1,2:T(8,128)} fusion(bf16[24,12,128]{0,1,2:T(8,128)(2,1)} %copy.50, bf16[24,96,128]{0,1,2:T(8,128)(2,1)S(1)} %copy.51), kind=kOutput, calls=%fused_computation.1 | convolution fusion | flops 7077888 | bytes 1253376 | tf_op jit(solution)/shard_map/kic,kjc->ijc/dot_general | solution.py:72
  97.0 2.7 %copy.52 = f32[96,12,128]{2,1,0:T(8,128)} copy(f32[96,12,128]{0,1,2:T(8,128)} %convolution_bitcast_fusion.1) | data formatting | bytes 1179648 | tf_op jit(solution)/shard_map/kic,kjc->ijc/transpose | solution.py:72
  99.7 25.0 %reduce-scatter.5.cloned.1.call-done = f32[24,12,128]{2,1,0:T(8,128)} async-done(((f32[96,12,128]{2,1,0:T(8,128)}), f32[24,12,128]{2,1,0:T(8,128)}) %reduce-scatter.5.cloned.1.call-update) | async-done | bytes 147472 | tf_op jit(solution)/shard_map/reduce_scatter | solution.py:11
  124.7 1.0 reduce_sum.78
  125.9 1.1 multiply_reduce_fusion
  127.3 1.1 add_convert_fusion
  128.5 1.6 %fusion.32 = bf16[24,12,128]{2,0,1:T(8,128)(2,1)} fusion(f32[24,12,128]{2,0,1:T(8,128)S(1)} %get-tuple-element.14, f32[24,12,128]{2,0,1:T(8,128)S(1)} %fusion.44, bf16[24,12,128]{2,0,1:T(8,128)(2,1)S(1)} %add_convert_fusion.1, bf16[2,5,128,128]{3,2,1,0:T(8,128)(2,1)} %param.8), kind=kOutput, calls=%fused_computation.40 | convolution fusion | flops 9658368 | bytes 475136 | tf_op jit(solution)/shard_map/dot_general | solution.py:28
  (23 shorter events, 1.0 us)
Async XLA Ops:
  6.5 55.8 %reduce-scatter.3.cloned.1.call-start = ((), (), s32[]{:S(2)}) async-start(), calls=%async_computation.2 | async-start | bytes 1327104 | tf_op jit(solution)/shard_map/reduce_scatter | solution.py:11
  26.7 37.8 %copy-start.1 = (bf16[2,128,128]{2,1,0:T(8,128)(2,1)S(1)}, bf16[2,128,128]{2,1,0:T(8,128)(2,1)}, u32[]{:S(2)}) copy-start(bf16[2,128,128]{2,1,0:T(8,128)(2,1)} %param.9) | copy-start | bytes 196612
  26.7 38.9 %copy-start = (bf16[24,12,128]{2,0,1:T(8,128)(2,1)S(1)}, bf16[24,12,128]{2,0,1:T(8,128)(2,1)}, u32[]{:S(2)}) copy-start(bf16[24,12,128]{2,0,1:T(8,128)(2,1)} %param.6) | copy-start | bytes 221188
  29.0 95.7 %reduce-scatter.5.cloned.1.call-start = ((), (), s32[]{:S(2)}) async-start(), calls=%async_computation.3 | async-start | bytes 983040 | tf_op jit(solution)/shard_map/reduce_scatter | solution.py:11
Sparse Core Ops, SparseCore 0:
  29.1 33.1 reduce-scatter.2
  99.9 24.7 reduce-scatter.4
where the time goes:
time: 138 us; the launch traced here: 137 us
  waiting for transfers between devices  58.3 us (42%)
  blocking collectives  26.8 us (19%)
  matrix products  16.9 us (12%)
  between operations  13.6 us (10%)
  local copies, waits for them, and re-layouts  12.7 us (9%)
  other arithmetic  8.57 us (6%)
    reduce_scatter x2, waiting for transfers between devices, scattered(): return lax.psum_scatter(whole, axis, scatter_dimension=0, tiled=True)  58.3 us
    all_gather x1, blocking collectives, shards(): left_all = lax.all_gather(left_side, 'col', axis=1, tiled=True)  15.8 us
    dot_general x10, matrix products, projections(): jnp.dot(flattened, proj_weight[layer_no, which], preferred_element_type=j...  11.2 us
    all_gather x1, blocking collectives, shards(): right_all = lax.all_gather(right_side, 'row', axis=0, tiled=True)  11 us
    all_gather x1, local copies, waits for them, and re-layouts, shards(): left_all = lax.all_gather(left_side, 'col', axis=1, tiled=True)  5.24 us
    dot_general x1, matrix products, incoming_term(): jnp.einsum('kic,kjc->ijc', sliced, right_side, preferred_element_type=jnp...  3.77 us
    reduce_sum x4, other arithmetic, layer_norm(): variance = jnp.mean(centred * centred, axis=-1, keepdims=True)  3.5 us
    reduce_sum x3, other arithmetic, layer_norm(): average = jnp.mean(values, axis=-1, keepdims=True)  3.06 us
  transfers between devices with their start and end apart: 2, of which 2 were waited for; matrix products, arithmetic and copies ran while one was open for 0% of the time, Pallas kernels for 0%

commit v1 on v0

--- a/solution.py
+++ b/solution.py
@@ -65,7 +65,8 @@
     left_side, right_side, gate_value = projections(
         pair_rep, mask_float, proj_weight, norm_gain, norm_bias, 1
     )
-    left_all = lax.all_gather(left_side, "col", axis=1, tiled=True)
+    blocks = lax.all_gather(left_side, "col")
+    left_all = jnp.concatenate(blocks, axis=1)
 
     def incoming_term(first_idx, how_many):
         sliced = lax.dynamic_slice_in_dim(left_all, first_idx, how_many, 1)

time: 138 us -> 121 us (0.88)
  matrix products: 16.9 us -> 8.13 us
  local copies, waits for them, and re-layouts: 12.7 us -> 6.11 us
    dot_general x10, matrix products: 11.2 us -> 5.73 us  [projections(): jnp.dot(flattened, proj_weight[layer_no, which], preferred_element_type=j...]
    all_gather x1, local copies, waits for them, and re-layouts: 5.24 us -> 0.06 us  [shards(): blocks = lax.all_gather(left_side, 'col')]
    dot_general x1, matrix products: 3.77 us -> 0.41 us  [incoming_term(): jnp.einsum('kic,kjc->ijc', sliced, right_side, preferred_element_type=jnp...]
where the time goes in v1:
time: 121 us
  waiting for transfers between devices  57.9 us (48%)
  blocking collectives  26.1 us (22%)
  between operations  13.7 us (11%)
  other arithmetic  8.63 us (7%)
  matrix products  8.13 us (7%)
  local copies, waits for them, and re-layouts  6.11 us (5%)
    reduce_scatter x2, waiting for transfers between devices, scattered(): return lax.psum_scatter(whole, axis, scatter_dimension=0, tiled=True)  57.9 us
    all_gather x1, blocking collectives, shards(): blocks = lax.all_gather(left_side, 'col')  15.1 us
    all_gather x1, blocking collectives, shards(): right_all = lax.all_gather(right_side, 'row', axis=0, tiled=True)  11 us
    dot_general x10, matrix products, projections(): jnp.dot(flattened, proj_weight[layer_no, which], preferred_element_type=j...  5.73 us
    reduce_sum x4, other arithmetic, layer_norm(): variance = jnp.mean(centred * centred, axis=-1, keepdims=True)  3.5 us
    reduce_sum x3, other arithmetic, layer_norm(): average = jnp.mean(values, axis=-1, keepdims=True)  3.12 us
  transfers between devices with their start and end apart: 2, of which 2 were waited for; matrix products, arithmetic and copies ran while one was open for 0% of the time, Pallas kernels for 0%

profile of v1, /device:TPU:0, one launch (start us, length us, event | category | flops | bytes accessed | tf_op | source)
XLA Modules:
  0.0 120.6 jit_solution(4517147775157252490)
XLA Ops:
  6.5 1.1 convert_reduce_fusion
  7.6 1.1 fusion.39
  8.7 0.8 slice_bitcast_fusion
  9.5 1.2 fusion.60
  10.7 1.2 fusion.57
  11.8 0.7 convert_element_type.43
  12.5 1.2 fusion.34
  13.7 0.3 fusion.33
  14.0 11.0 %all_gather.9 = bf16[96,12,128]{2,0,1:T(8,128)(2,1)S(1)} all-gather(bf16[24,12,128]{2,0,1:T(8,128)(2,1)S(1)} %fusion.33), channel_id=1, replica_groups=mesh['row'=4,'col'=8] {'row'}, dimensions={0}, use_global_device_ids=true | all-gather | bytes 368640 | tf_op jit(solution)/shard_map/all_gather | solution.py:56
  25.0 0.4 copy.55
  25.5 0.4 copy.54
  25.9 0.6 convolution_bitcast_fusion
  26.6 1.6 %copy.56 = f32[96,24,128]{2,1,0:T(8,128)} copy(f32[96,24,128]{0,1,2:T(8,128)S(1)} %convolution_bitcast_fusion) | data formatting | bytes 2359296 | tf_op jit(solution)/shard_map/jkc,ikc->jic/transpose | solution.py:60
  28.2 33.3 %reduce-scatter.3.cloned.1.call-done = f32[12,24,128]{2,1,0:T(8,128)} async-done(((f32[96,24,128]{2,1,0:T(8,128)}), f32[12,24,128]{2,1,0:T(8,128)}) %reduce-scatter.3.cloned.1.call-update) | async-done | bytes 147472 | tf_op jit(solution)/shard_map/reduce_scatter | solution.py:11
  61.5 1.0 bitcast_reduce_fusion
  62.6 1.1 multiply_reduce_fusion.2
  63.7 1.2 fusion.43
  64.9 0.4 fusion.83
  65.3 0.2 multiply_reduce_fusion.1
  65.8 0.2 fusion.53
  66.0 0.2 fusion.30
  66.2 0.2 fusion.31
  66.4 0.4 copy.62
  66.8 15.1 %all-gather = bf16[192,12,128]{2,0,1:T(8,128)(2,1)S(1)} all-gather(bf16[24,12,128]{2,0,1:T(8,128)(2,1)S(1)} %fusion.30), channel_id=2, replica_groups=mesh['row'=4,'col'=8] {'col'}, dimensions={0}, use_global_device_ids=true | all-gather | bytes 663552 | tf_op jit(solution)/shard_map/all_gather | solution.py:68
  82.0 0.6 copy.63
  82.6 0.4 convolution_bitcast_fusion.1
  83.0 1.5 %copy.64 = f32[96,12,128]{2,1,0:T(8,128)} copy(f32[96,12,128]{0,1,2:T(8,128)S(1)} %convolution_bitcast_fusion.1) | data formatting | bytes 1179648 | tf_op jit(solution)/shard_map/kic,kjc->ijc/transpose | solution.py:73
  84.5 24.6 %reduce-scatter.5.cloned.1.call-done = f32[24,12,128]{2,1,0:T(8,128)} async-done(((f32[96,12,128]{2,1,0:T(8,128)}), f32[24,12,128]{2,1,0:T(8,128)}) %reduce-scatter.5.cloned.1.call-update) | async-done | bytes 147472 | tf_op jit(solution)/shard_map/reduce_scatter | solution.py:11
  109.1 1.0 reduce_sum.78
  110.3 1.1 multiply_reduce_fusion
  111.7 1.1 add_convert_fusion
  112.9 0.8 fusion.32
  (26 shorter events, 1.0 us)
Async XLA Ops:
  6.5 7.2 %copy-start = (bf16[24,12,128]{2,0,1:T(8,128)(2,1)S(1)}, bf16[24,12,128]{2,0,1:T(8,128)(2,1)}, u32[]{:S(2)}) copy-start(bf16[24,12,128]{2,0,1:T(8,128)(2,1)} %param.6) | copy-start | bytes 221188
  6.5 7.2 %copy-start.2 = (bf16[2,5,128,128]{3,2,1,0:T(8,128)(2,1)S(1)}, bf16[2,5,128,128]{3,2,1,0:T(8,128)(2,1)}, u32[]{:S(2)}) copy-start(bf16[2,5,128,128]{3,2,1,0:T(8,128)(2,1)} %param.8) | copy-start | bytes 983044
  6.5 55.0 %reduce-scatter.3.cloned.1.call-start = ((), (), s32[]{:S(2)}) async-start(), calls=%async_computation.2 | async-start | bytes 1327104 | tf_op jit(solution)/shard_map/reduce_scatter | solution.py:11
  26.6 37.1 %copy-start.1 = (bf16[2,128,128]{2,1,0:T(8,128)(2,1)S(1)}, bf16[2,128,128]{2,1,0:T(8,128)(2,1)}, u32[]{:S(2)}) copy-start(bf16[2,128,128]{2,1,0:T(8,128)(2,1)} %param.9) | copy-start | bytes 196612
  28.1 81.0 %reduce-scatter.5.cloned.1.call-start = ((), (), s32[]{:S(2)}) async-start(), calls=%async_computation.3 | async-start | bytes 983040 | tf_op jit(solution)/shard_map/reduce_scatter | solution.py:11
Sparse Core Ops, SparseCore 0:
  28.3 33.2 reduce-scatter.2
  84.6 24.4 reduce-scatter.4
